TPU v7x, 32 devices: a whole 2x2x4 slice. The times are simulated.
32 devices in a mesh: hi: 16 (over z, x, core), grp: 2 (over y).
Axes of the slice: x: 2, y: 2, z: 4, core: 2. Of those that a mesh axis runs over, the one named last changes fastest.
Arguments:
- rho: float32 [2, 8192, 8192], P(None, ('hi', 'grp')), may hold values from -6 to 9
- perm: int32 [2, 13], replicated, may hold values from 0 to 12, each once within a row
- superop: float32 [2, 2, 16, 16], replicated, may hold values from -0.3 to 1.1
Outputs:
- rho_out: float32 [2, 8192, 8192], P(None, ('hi', 'grp'))
- trace_mean: float32 [], replicated
All inputs are finite; a program needn't handle non-finite values.
Results may differ from a plain program's by a relative error of at most 0.0001.
Values sent between devices are 32-bit elements; how exact they have to be, the bound alone decides.
A program may use at most 384 MiB of HBM per device.

v0:
```python
import jax
import jax.numpy as jnp
from jax import lax
from jax.experimental import pallas as pl
from jax.experimental.pallas import tpu as pltpu
from jax.sharding import PartitionSpec as P

PAIRS = 2
SPAN = 4**PAIRS
AXES = ("hi", "grp")
VMEM_LIMIT = 60 * 1024 * 1024


def relabel_table(order, count):
    positions = jnp.arange(count, dtype=jnp.int32)
    result = jnp.zeros((count,), jnp.int32)
    for qubit in range(order.shape[0]):
        bit_value = jnp.bitwise_and(jnp.right_shift(positions, qubit), 1)
        result = result + bit_value * jnp.left_shift(jnp.int32(1), order[qubit])
    return result


def gather_body(idx_ref, x_ref, o_ref):
    rows = o_ref.shape[0]
    base = pl.program_id(0) * rows

    @pl.loop(0, rows // 8)
    def _(block):
        start = pl.multiple_of(block * 8, 8)
        for k in range(8):
            src = idx_ref[base + start + k]
            o_ref[pl.ds(start + k, 1), :] = x_ref[pl.ds(src, 1), :]


def gather_rows(x, idx):
    count, width = x.shape
    rows = 512
    return pl.pallas_call(
        gather_body,
        out_shape=jax.ShapeDtypeStruct(x.shape, x.dtype),
        grid_spec=pltpu.PrefetchScalarGridSpec(
            num_scalar_prefetch=1,
            grid=(count // rows,),
            in_specs=[
                pl.BlockSpec((count, width), lambda i, s: (0, 0), pipeline_mode=pl.Buffered(1))
            ],
            out_specs=pl.BlockSpec((rows, width), lambda i, s: (i, 0)),
        ),
        compiler_params=pltpu.CompilerParams(vmem_limit_bytes=VMEM_LIMIT),
        name="gather_rows",
    )(idx, x)


def gather_turn_body(idx_ref, x_ref, o_ref, tmp):
    rows = tmp.shape[0]
    low = pl.program_id(0)

    @pl.loop(0, rows // 8)
    def _(block):
        start = pl.multiple_of(block * 8, 8)
        for k in range(8):
            src = idx_ref[(start + k) * SPAN + low]
            tmp[pl.ds(start + k, 1), :] = x_ref[pl.ds(src, 1), :]

    o_ref[0] = tmp[...].T


def gather_turn(x, idx):
    count, width = x.shape
    rows = count // SPAN
    return pl.pallas_call(
        gather_turn_body,
        out_shape=jax.ShapeDtypeStruct((SPAN, width, rows), x.dtype),
        grid_spec=pltpu.PrefetchScalarGridSpec(
            num_scalar_prefetch=1,
            grid=(SPAN,),
            in_specs=[
                pl.BlockSpec((count, width), lambda i, s: (0, 0), pipeline_mode=pl.Buffered(1))
            ],
            out_specs=pl.BlockSpec((1, width, rows), lambda i, s: (i, 0, 0)),
            scratch_shapes=[pltpu.VMEM((rows, width), x.dtype)],
        ),
        compiler_params=pltpu.CompilerParams(vmem_limit_bytes=VMEM_LIMIT),
        name="gather_turn",
    )(idx, x)


def channel_body(kernel_ref, x_ref, o_ref):
    block = x_ref[...].reshape(2 * SPAN * SPAN, x_ref.shape[-1])
    mixed = jnp.dot(
        kernel_ref[...],
        block,
        precision=lax.Precision.HIGHEST,
        preferred_element_type=jnp.float32,
    )
    o_ref[...] = mixed.reshape(o_ref.shape)


def apply_channel(x, kernel):
    span, width, lanes = x.shape
    blocks = width // (2 * SPAN)
    shaped = x.reshape(span, 2, blocks, SPAN, lanes)
    side = 2 * SPAN * SPAN
    spec = pl.BlockSpec((span, 2, 1, SPAN, lanes), lambda i: (0, 0, i, 0, 0))
    whole = pl.BlockSpec((side, side), lambda i: (0, 0))
    out = pl.pallas_call(
        channel_body,
        out_shape=jax.ShapeDtypeStruct(shaped.shape, x.dtype),
        grid=(blocks,),
        in_specs=[whole, spec],
        out_specs=spec,
        compiler_params=pltpu.CompilerParams(vmem_limit_bytes=VMEM_LIMIT),
        name="channel",
    )(kernel, shaped)
    return out.reshape(x.shape)


def pair_kernel(layer_super):
    real = layer_super[0].reshape(4, 4, 4, 4)
    imag = layer_super[1].reshape(4, 4, 4, 4)

    def outer(a, b):
        both = a[:, None, :, None, :, None, :, None] * b[None, :, None, :, None, :, None, :]
        return both.reshape(SPAN, SPAN, SPAN, SPAN)

    re = outer(real, real) - outer(imag, imag)
    im = outer(real, imag) + outer(imag, real)
    top = jnp.stack([re, -im], axis=2)
    bottom = jnp.stack([im, re], axis=2)
    return jnp.stack([top, bottom], axis=0)


def exchange(x):
    return lax.all_to_all(x, AXES, split_axis=0, concat_axis=0, tiled=True)


def swap_local(x, local):
    shaped = x.reshape(x.shape[0] // local, local, 2, local)
    return jnp.transpose(shaped, (0, 3, 2, 1)).reshape(x.shape)


def per_device(rho, perm, superop):
    full = rho.shape[2]
    local = rho.shape[1]
    side = 2 * SPAN * SPAN
    table0 = relabel_table(perm[0], full)
    table1 = relabel_table(perm[1], full)
    kernel0 = jnp.transpose(pair_kernel(superop[0]), (1, 0, 2, 4, 3, 5)).reshape(side, side)
    kernel1 = jnp.transpose(pair_kernel(superop[1]), (2, 0, 1, 5, 3, 4)).reshape(side, side)

    x = rho.reshape(2 * local, full).T
    x = gather_rows(x, table0)
    x = exchange(x)
    x = swap_local(x, local)
    x = gather_turn(x, table0)
    x = apply_channel(x, kernel0)
    x = jnp.transpose(x, (2, 0, 1)).reshape(full, 2 * local)
    x = gather_rows(x, table1)
    x = exchange(x)
    x = swap_local(x, local)
    x = gather_turn(x, table1)
    x = apply_channel(x, kernel1)
    x = jnp.transpose(x, (2, 0, 1)).reshape(full, 2 * local)
    matrix = x.T.reshape(2, local, full)

    position = lax.axis_index(AXES)
    diagonal_block = lax.dynamic_slice_in_dim(matrix[0], position * local, local, 1)
    trace_total = lax.psum(jnp.trace(diagonal_block), AXES)
    return (matrix, trace_total / full)


def solution(mesh):
    assert PAIRS == 2
    placed = (P(None, AXES, None), P(), P())
    return jax.shard_map(
        per_device,
        mesh=mesh,
        in_specs=placed,
        out_specs=(P(None, AXES, None), P()),
        check_vma=False,
    )
```

profile of v0, /device:TPU:0, one launch (start us, length us, event | category | flops | bytes accessed | tf_op | source)
XLA Modules:
  0.0 1236.3 jit_solution(10433097013111649665)
XLA Ops:
  0.6 1.6 fusion.2
  2.2 2.1 fusion.1
  12.5 17.4 %copy.27 = f32[512,8192]{0,1:T(8,128)} copy(f32[512,8192]{1,0:T(8,128)} %bitcast.97) | data formatting | bytes 33554432 | tf_op jit(solution)/shard_map/reshape | solution.py:151
  30.0 0.7 multiply_add_fusion.2.idx_ref
  30.6 39.6 %gather_rows.2 = f32[8192,512]{1,0:T(8,128)} custom-call(s32[8192]{0:T(1024)} %multiply_add_fusion.2.idx_ref, f32[8192,512]{1,0:T(8,128)} %bitcast.85), custom_call_target="tpu_custom_call" | custom-call | tf_op jit(solution)/shard_map/gather_rows/pallas_call | solution.py:38
  70.2 17.4 %copy.20 = f32[32,256,512]{1,2,0:T(8,128)} copy(f32[32,256,512]{2,1,0:T(8,128)} %bitcast.90) | data formatting | bytes 33554432 | tf_op jit(solution)/shard_map/all_to_all | solution.py:134
  87.6 0.0 copy-start
  87.6 7.5 all-to-all-start
  103.0 0.0 copy-done
  103.1 0.1 mul.382
  103.2 0.1 mul.386
  103.2 7.8 multiply_add_fusion
  111.0 7.8 add.129
  118.8 3.5 neg.21
  122.3 8.8 sub.29
  131.1 11.1 maximum_bitcast_fusion.4
  142.1 5.5 maximum_bitcast_fusion.1
  147.7 13.5 %reshape.402.kernel_ref = f32[512,512]{1,0:T(8,128)} reshape(f32[16,2,16,16,2,16]{5,4,3,2,1,0:T(2,128)} %maximum_bitcast_fusion.1) | data formatting | bytes 2097152 | tf_op jit(solution)/shard_map/reshape | solution.py:148
  161.2 0.7 multiply_add_fusion.3.idx_ref
  161.8 303.6 %all-to-all-done = f32[32,256,512]{1,2,0:T(8,128)} async-done(((f32[32,256,512]{1,2,0:T(8,128)}), f32[32,256,512]{1,2,0:T(8,128)}, u32[]{:S(2)}, u32[]{:S(2)}) %all-to-all-start) | async-done | bytes 16777248 | tf_op jit(solution)/shard_map/all_to_all | solution.py:134
  465.5 27.4 %copy.21 = f32[32,256,2,256]{3,2,1,0:T(2,128)S(1)} copy(f32[32,256,2,256]{3,1,2,0:T(8,128)} %bitcast.38) | data formatting | bytes 33554432 | tf_op jit(solution)/shard_map/transpose | solution.py:139
  492.9 7.3 copy.29
  500.2 46.9 %gather_turn.2 = f32[16,512,512]{2,1,0:T(8,128)} custom-call(s32[8192]{0:T(1024)} %multiply_add_fusion.2.idx_ref, f32[8192,512]{1,0:T(8,128)} %bitcast.88), custom_call_target="tpu_custom_call" | custom-call | tf_op jit(solution)/shard_map/gather_turn/pallas_call | solution.py:71
  547.1 32.2 %channel.2 = f32[16,2,16,16,512]{4,3,2,1,0:T(8,128)} custom-call(f32[512,512]{1,0:T(8,128)} %reshape.402.kernel_ref, f32[16,2,16,16,512]{4,3,2,1,0:T(8,128)} %bitcast.86), custom_call_target="tpu_custom_call" | custom-call | tf_op jit(solution)/shard_map/channel/pallas_call | solution.py:106
  579.3 20.2 %copy.22 = f32[16,512,512]{1,0,2:T(8,128)} copy(f32[16,512,512]{2,1,0:T(8,128)} %bitcast.93) | data formatting | bytes 33554432 | tf_op jit(solution)/shard_map/reshape | solution.py:115
  599.5 39.5 %gather_rows.3 = f32[8192,512]{1,0:T(8,128)} custom-call(s32[8192]{0:T(1024)} %multiply_add_fusion.3.idx_ref, f32[8192,512]{1,0:T(8,128)} %bitcast.91), custom_call_target="tpu_custom_call" | custom-call | tf_op jit(solution)/shard_map/gather_rows/pallas_call | solution.py:38
  639.0 17.4 %copy.23 = f32[32,256,512]{1,2,0:T(8,128)} copy(f32[32,256,512]{2,1,0:T(8,128)} %bitcast.92) | data formatting | bytes 33554432 | tf_op jit(solution)/shard_map/all_to_all | solution.py:134
  656.5 8.6 all-to-all-start.1
  665.1 0.1 mul.350
  665.2 0.2 copy.15
  665.4 0.1 mul.346
  665.5 0.2 copy.13
  665.7 7.8 multiply_add_fusion.1
  673.5 7.8 add.115
  681.3 3.5 neg.20
  684.8 8.8 sub.27
  693.6 11.1 maximum_bitcast_fusion.2
  704.7 5.5 maximum_bitcast_fusion
  710.2 13.6 %reshape.401.kernel_ref = f32[512,512]{1,0:T(8,128)} reshape(f32[16,2,16,16,2,16]{5,4,3,2,1,0:T(2,128)} %maximum_bitcast_fusion) | data formatting | bytes 2097152 | tf_op jit(solution)/shard_map/reshape | solution.py:149
  723.8 311.7 %all-to-all-done.1 = f32[32,256,512]{1,2,0:T(8,128)} async-done(((f32[32,256,512]{1,2,0:T(8,128)}), f32[32,256,512]{1,2,0:T(8,128)}, u32[]{:S(2)}, u32[]{:S(2)}) %all-to-all-start.1) | async-done | bytes 16777248 | tf_op jit(solution)/shard_map/all_to_all | solution.py:134
  1035.5 27.4 %copy.24 = f32[32,256,2,256]{3,2,1,0:T(2,128)S(1)} copy(f32[32,256,2,256]{3,1,2,0:T(8,128)} %bitcast.45) | data formatting | bytes 33554432 | tf_op jit(solution)/shard_map/transpose | solution.py:139
  1063.0 7.3 copy.30
  1070.2 46.9 %gather_turn.3 = f32[16,512,512]{2,1,0:T(8,128)} custom-call(s32[8192]{0:T(1024)} %multiply_add_fusion.3.idx_ref, f32[8192,512]{1,0:T(8,128)} %bitcast.89), custom_call_target="tpu_custom_call" | custom-call | tf_op jit(solution)/shard_map/gather_turn/pallas_call | solution.py:71
  1117.1 32.2 %channel.3 = f32[16,2,16,16,512]{4,3,2,1,0:T(8,128)} custom-call(f32[512,512]{1,0:T(8,128)} %reshape.401.kernel_ref, f32[16,2,16,16,512]{4,3,2,1,0:T(8,128)} %bitcast.87), custom_call_target="tpu_custom_call" | custom-call | tf_op jit(solution)/shard_map/channel/pallas_call | solution.py:106
  1149.3 20.2 %copy.25 = f32[16,512,512]{1,0,2:T(8,128)} copy(f32[16,512,512]{2,1,0:T(8,128)} %bitcast.94) | data formatting | bytes 33554432 | tf_op jit(solution)/shard_map/reshape | solution.py:115
  1169.5 4.0 slice.189
  1173.5 0.6 select_reduce_fusion
  1174.1 17.4 %copy.28 = f32[512,8192]{1,0:T(8,128)} copy(f32[512,8192]{0,1:T(8,128)} %bitcast.84) | data formatting | bytes 33554432
  1191.6 42.5 %psum.7 = f32[]{:T(128)} all-reduce(f32[]{:T(128)} %select_reduce_fusion), channel_id=1, replica_groups=mesh['hi'=16,'grp'=2] {'hi','grp'}, use_global_device_ids=true, to_apply=%region_1.2 | all-reduce | flops 1 | bytes 8 | tf_op jit(solution)/shard_map/psum | solution.py:168
  (1 shorter events, 0.0 us)
Async XLA Ops:
  87.6 15.4 %copy-start = (f32[2,2,16,16]{3,2,1,0:T(8,128)S(1)}, f32[2,2,16,16]{3,2,1,0:T(8,128)}, u32[]{:S(2)}) copy-start(f32[2,2,16,16]{3,2,1,0:T(8,128)} %param.5) | copy-start | bytes 12292
  87.6 377.8 %all-to-all-start = ((f32[32,256,512]{1,2,0:T(8,128)}), f32[32,256,512]{1,2,0:T(8,128)}, u32[]{:S(2)}, u32[]{:S(2)}) async-start(f32[32,256,512]{1,2,0:T(8,128)} %copy.20), calls=%async_computation | async-start | bytes 33554432 | tf_op jit(solution)/shard_map/all_to_all | solution.py:134
  656.5 379.0 %all-to-all-start.1 = ((f32[32,256,512]{1,2,0:T(8,128)}), f32[32,256,512]{1,2,0:T(8,128)}, u32[]{:S(2)}, u32[]{:S(2)}) async-start(f32[32,256,512]{1,2,0:T(8,128)} %copy.23), calls=%async_computation.1 | async-start | bytes 33554432 | tf_op jit(solution)/shard_map/all_to_all | solution.py:134
where the time goes:
time: 1250 us; the launch traced here: 1240 us
  waiting for transfers between devices  615 us (49%)
  local copies, waits for them, and re-layouts  248 us (20%)
  Pallas kernels  237 us (19%)
  other arithmetic  57.8 us (5%)
  blocking collectives  42.5 us (3%)
  between operations  19.1 us (2%)
  starting transfers between devices  16.1 us (1%)
    all_to_all x2, waiting for transfers between devices, exchange(): return lax.all_to_all(x, AXES, split_axis=0, concat_axis=0, tiled=True)  615 us
    pallas_call x2, Pallas kernels, gather_turn(): pl.pallas_call(gather_turn_body, out_shape=jax.ShapeDtypeStruct((SPAN, wi...  93.8 us
    pallas_call x2, Pallas kernels, gather_rows(): pl.pallas_call(gather_body, out_shape=jax.ShapeDtypeStruct(x.shape, x.dty...  79.1 us
    pallas_call x2, Pallas kernels, apply_channel(): pl.pallas_call(channel_body, out_shape=jax.ShapeDtypeStruct(shaped.shape,...  64.4 us
    transpose x2, local copies, waits for them, and re-layouts, swap_local(): return jnp.transpose(shaped, (0, 3, 2, 1)).reshape(x.shape)  54.9 us
    psum x1, blocking collectives, per_device(): trace_total = lax.psum(jnp.trace(diagonal_block), AXES)  42.5 us
    reshape x2, local copies, waits for them, and re-layouts, apply_channel(): return out.reshape(x.shape)  40.4 us
    all_to_all x2, local copies, waits for them, and re-layouts, exchange(): return lax.all_to_all(x, AXES, split_axis=0, concat_axis=0, tiled=True)  34.9 us
  transfers between devices with their start and end apart: 2, of which 2 were waited for; matrix products, arithmetic and copies ran while one was open for 9% of the time, Pallas kernels for 0%

commit v1 on v0

--- a/solution.py
+++ b/solution.py
@@ -1,3 +1,5 @@
+import functools
+
 import jax
 import jax.numpy as jnp
 from jax import lax
@@ -9,6 +11,8 @@
 SPAN = 4**PAIRS
 AXES = ("hi", "grp")
 VMEM_LIMIT = 60 * 1024 * 1024
+LANES = 128
+SIDE = 2 * SPAN * SPAN
 
 
 def relabel_table(order, count):
@@ -139,7 +143,7 @@
     return jnp.transpose(shaped, (0, 3, 2, 1)).reshape(x.shape)
 
 
-def per_device(rho, perm, superop):
+def simple_per_device(rho, perm, superop):
     full = rho.shape[2]
     local = rho.shape[1]
     side = 2 * SPAN * SPAN
@@ -163,9 +167,267 @@
     x = jnp.transpose(x, (2, 0, 1)).reshape(full, 2 * local)
     matrix = x.T.reshape(2, local, full)
 
+    return matrix
+
+
+def params():
+    return pltpu.CompilerParams(vmem_limit_bytes=VMEM_LIMIT)
+
+
+def cost(flops, nbytes):
+    return pl.CostEstimate(flops=flops, bytes_accessed=nbytes, transcendentals=0)
+
+
+def whole():
+    return pl.BlockSpec(memory_space=pltpu.VMEM)
+
+
+def copy_rows(idx_ref, first, step, count, parts, src_ref, dst_ref, base):
+    @pl.loop(0, count // 16)
+    def _(block):
+        start = block * 16
+        for k in range(16):
+            src = pl.multiple_of(idx_ref[first + step * (start + k)] * parts, parts)
+            dst = pl.multiple_of((base + start + k) * parts, parts)
+            dst_ref[pl.ds(dst, parts), :] = src_ref[pl.ds(src, parts), :]
+
+
+def turn_body(x_ref, o_ref):
+    parts = x_ref.shape[0] // LANES
+    cols = x_ref.shape[1]
+    for k in range(parts):
+        o_ref[pl.ds(k, cols, stride=parts), :] = x_ref[pl.ds(k * LANES, LANES), :].T
+
+
+def turn(x):
+    height, full = x.shape
+    parts = height // LANES
+    cols = 512
+    return pl.pallas_call(
+        turn_body,
+        out_shape=jax.ShapeDtypeStruct((full * parts, LANES), x.dtype),
+        grid=(full // cols,),
+        in_specs=[pl.BlockSpec((height, cols), lambda i: (0, i))],
+        out_specs=pl.BlockSpec((cols * parts, LANES), lambda i: (i, 0)),
+        compiler_params=params(),
+        cost_estimate=cost(10**8, 2 * x.size * 4),
+        name="turn",
+    )(x)
+
+
+def pick_body(chunk, local, parts, idx_ref, x_ref, o_ref):
+    first = pl.program_id(0) * local + chunk * LANES
+    copy_rows(idx_ref, first, 1, LANES, parts, x_ref, o_ref.at[0], 0)
+
+
+def pick(xt, table, chunk, local, devices):
+    parts = xt.shape[0] // (devices * local)
+    return pl.pallas_call(
+        functools.partial(pick_body, chunk, local, parts),
+        out_shape=jax.ShapeDtypeStruct((devices, LANES * parts, LANES), xt.dtype),
+        grid_spec=pltpu.PrefetchScalarGridSpec(
+            num_scalar_prefetch=1,
+            grid=(devices,),
+            in_specs=[whole()],
+            out_specs=pl.BlockSpec((1, LANES * parts, LANES), lambda i, s: (i, 0, 0)),
+        ),
+        compiler_params=params(),
+        cost_estimate=cost(10**8, 3 * xt.size * 4),
+        name="pick",
+    )(table, xt)
+
+
+def mix(idx_ref, w_ref, g, xk, tmp):
+    high = tmp.shape[0] // 2
+    groups = LANES // SPAN
+
+    @pl.loop(0, SPAN)
+    def _(low):
+        copy_rows(idx_ref, low, SPAN, high, 2, g, tmp, 0)
+        for part in range(2):
+            turned = tmp[pl.ds(part, high, stride=2), :].T
+            at = pl.multiple_of(low * 2 * SPAN + part * SPAN, SPAN)
+            xk[:, pl.ds(at, SPAN), :] = turned.reshape(groups, SPAN, high)
+
+    w = w_ref[...]
+    w_big = w.astype(jnp.bfloat16)
+    w_small = (w - w_big.astype(jnp.float32)).astype(jnp.bfloat16)
+
+    @pl.loop(0, groups)
+    def _(group):
+        x = xk[group]
+        x_big = x.astype(jnp.bfloat16)
+        x_small = (x - x_big.astype(jnp.float32)).astype(jnp.bfloat16)
+        y = jnp.dot(w_big, x_small, preferred_element_type=jnp.float32)
+        y += jnp.dot(w_small, x_big, preferred_element_type=jnp.float32)
+        y += jnp.dot(w_big, x_big, preferred_element_type=jnp.float32)
+        xk[group] = y
+
+
+def middle_body(local, idx_ref, next_ref, w_ref, r_ref, *refs):
+    *outs, g, xk, tmp = refs
+    devices = r_ref.shape[0]
+    parts = r_ref.shape[1] // LANES
+    halves = parts // 2
+    high = tmp.shape[0] // 2
+
+    @pl.loop(0, devices)
+    def _(s):
+        for k in range(parts):
+            part, half = k // halves, k % halves
+            block = r_ref[s, pl.ds(k, LANES, stride=parts), :]
+            at = (s * local + half * LANES) * 2 + part
+            g[pl.ds(at, LANES, stride=2), :] = block.T
+
+    mix(idx_ref, w_ref, g, xk, tmp)
+
+    @pl.loop(0, SPAN)
+    def _(low):
+        for part in range(2):
+            at = pl.multiple_of(low * 2 * SPAN + part * SPAN, SPAN)
+            block = xk[:, pl.ds(at, SPAN), :].reshape(LANES, high)
+            g[pl.ds(low * high * 2 + part, high, stride=2), :] = block.T
+
+    @pl.loop(0, devices)
+    def _(d):
+        for b, out in enumerate(outs):
+            copy_rows(next_ref, d * local + b * LANES, 1, LANES, 2, g, out.at[d], 0)
+
+
+def middle(r, table, next_table, w, local):
+    devices = r.shape[0]
+    full = devices * local
+    high = full // SPAN
+    message = jax.ShapeDtypeStruct((devices, 2 * LANES, LANES), r.dtype)
+    count = local // LANES
+    return pl.pallas_call(
+        functools.partial(middle_body, local),
+        out_shape=[message] * count,
+        in_specs=[
+            pl.BlockSpec(memory_space=pltpu.SMEM),
+            pl.BlockSpec(memory_space=pltpu.SMEM),
+            whole(),
+            whole(),
+        ],
+        out_specs=[whole()] * count,
+        scratch_shapes=[
+            pltpu.VMEM((full * 2, LANES), r.dtype),
+            pltpu.VMEM((LANES // SPAN, SIDE, high), r.dtype),
+            pltpu.VMEM((high * 2, LANES), r.dtype),
+        ],
+        compiler_params=params(),
+        cost_estimate=cost(2 * 3 * SIDE * full * 2 * LANES, 2 * r.size * 4),
+        name="middle",
+    )(table, next_table, w, r)
+
+
+def last_body(local, count, idx_ref, w_ref, *refs):
+    rs = refs[:count]
+    o_ref, g, xk, tmp = refs[-4:]
+    devices = rs[0].shape[0]
+    full = devices * local
+    high = tmp.shape[0] // 2
+    step = pl.program_id(0)
+
+    @pl.when(step == 0)
+    def _():
+        @pl.loop(0, devices)
+        def _(s):
+            for a, r_ref in enumerate(rs):
+                for part in range(2):
+                    block = r_ref[s, pl.ds(part, LANES, stride=2), :]
+                    at = (s * local + a * LANES) * 2 + part
+                    g[pl.ds(at, LANES, stride=2), :] = block.T
+
+        mix(idx_ref, w_ref, g, xk, tmp)
+
+        @pl.loop(0, SPAN)
+        def _(low):
+            for part in range(2):
+                at = pl.multiple_of(low * 2 * SPAN + part * SPAN, SPAN)
+                block = xk[:, pl.ds(at, SPAN), :].reshape(LANES, high)
+                g[pl.ds(part * full + low, high, stride=SPAN), :] = block.T
+
+    cols = o_ref.shape[2]
+    for part in range(2):
+        at = pl.multiple_of(part * full + step * cols, LANES)
+        o_ref[part] = g[pl.ds(at, cols), :].T
+
+
+def last(rs, table, w, local, which, before):
+    devices = rs[0].shape[0]
+    full = devices * local
+    high = full // SPAN
+    cols = 1024
+    count = len(rs)
+    extra = [] if before is None else [before]
+    return pl.pallas_call(
+        functools.partial(last_body, local, count),
+        out_shape=jax.ShapeDtypeStruct((2, local, full), rs[0].dtype),
+        grid=(full // cols,),
+        in_specs=[pl.BlockSpec(memory_space=pltpu.SMEM), whole()]
+        + [whole()] * count
+        + [pl.BlockSpec(memory_space=pl.ANY)] * len(extra),
+        out_specs=pl.BlockSpec((2, LANES, cols), lambda i: (0, which, i)),
+        scratch_shapes=[
+            pltpu.VMEM((full * 2, LANES), rs[0].dtype),
+            pltpu.VMEM((LANES // SPAN, SIDE, high), rs[0].dtype),
+            pltpu.VMEM((high * 2, LANES), rs[0].dtype),
+        ],
+        input_output_aliases={2 + count: 0} if extra else {},
+        compiler_params=params(),
+        cost_estimate=cost(2 * 3 * SIDE * full * 2 * LANES, 4 * full * 2 * LANES * 4),
+        name="last",
+    )(table, w, *rs, *extra)
+
+
+def sum_over_devices(value, devices):
+    copies = jnp.full((devices, LANES), value, value.dtype)
+    return jnp.sum(exchange(copies)[:, 0])
+
+
+def after(x, *done):
+    return lax.optimization_barrier((x, *done))[0]
+
+
+def chunked_per_device(rho, perm, superop):
+    full = rho.shape[2]
+    local = rho.shape[1]
+    devices = full // local
+    count = local // LANES
+    table0 = relabel_table(perm[0], full)
+    table1 = relabel_table(perm[1], full)
+    spread1 = (table1 % SPAN) * (full // SPAN) + table1 // SPAN
+    kernel0 = jnp.transpose(pair_kernel(superop[0]), (1, 0, 2, 4, 3, 5)).reshape(SIDE, SIDE)
+    kernel1 = jnp.transpose(pair_kernel(superop[1]), (2, 0, 1, 5, 3, 4)).reshape(SIDE, SIDE)
+
+    xt = turn(rho.reshape(2 * local, full))
+    got = []
+    for a in range(count):
+        message = pick(xt, table0, a, local, devices)
+        got.append(exchange(after(message, *got[-1:])))
+    done = got[-1]
+    parts = [[] for _ in range(count)]
+    for a in range(count):
+        messages = middle(got[a], table0, spread1, kernel0, local)
+        for b, message in enumerate(messages):
+            done = exchange(after(message, done))
+            parts[b].append(done)
+    matrix = None
+    for b in range(count):
+        matrix = last(parts[b], table1, kernel1, local, b, matrix)
+    return matrix
+
+
+def per_device(rho, perm, superop):
+    full = rho.shape[2]
+    local = rho.shape[1]
+    run = simple_per_device if local % LANES else chunked_per_device
+    matrix = run(rho, perm, superop)
+
     position = lax.axis_index(AXES)
     diagonal_block = lax.dynamic_slice_in_dim(matrix[0], position * local, local, 1)
-    trace_total = lax.psum(jnp.trace(diagonal_block), AXES)
+    trace_total = sum_over_devices(jnp.trace(diagonal_block), full // local)
     return (matrix, trace_total / full)
 
 

time: 1250 us -> 903 us (0.72)
  waiting for transfers between devices: 615 us -> 273 us
  local copies, waits for them, and re-layouts: 248 us -> 68.8 us
  blocking collectives: 42.5 us -> 208 us
  Pallas kernels: 237 us -> 254 us
    all_to_all x2 -> x4, waiting for transfers between devices: 615 us -> 273 us  [exchange(): return lax.all_to_all(x, AXES, split_axis=0, concat_axis=0, tiled=True)]
    all_to_all x0 -> x3, blocking collectives: none -> 208 us  [exchange(): return lax.all_to_all(x, AXES, split_axis=0, concat_axis=0, tiled=True)]
    reshape x5 -> x2, local copies, waits for them, and re-layouts: 84.9 us -> 26.7 us  [the longest x1 13.4 us: chunked_per_device(): jnp.transpose(pair_kernel(superop[0]), (1, 0, 2, 4, 3, 5))]
    transpose x2 -> x0, local copies, waits for them, and re-layouts: 54.9 us -> none  [swap_local(): return jnp.transpose(shaped, (0, 3, 2, 1)).reshape(x.shape)]
    psum x1 -> x0, blocking collectives: 42.5 us -> none  [per_device(): trace_total = lax.psum(jnp.trace(diagonal_block), AXES)]
    all_to_all x2 -> x0, local copies, waits for them, and re-layouts: 34.9 us -> none  [exchange(): return lax.all_to_all(x, AXES, split_axis=0, concat_axis=0, tiled=True)]
    unnamed x5 -> x2, local copies, waits for them, and re-layouts: 32 us -> 0.01 us
    pallas_call x6 -> x7, Pallas kernels: 237 us -> 254 us  [the longest x2 105 us: middle(): pl.pallas_call(functools.partial(middle_body, local), out_shape=[message]...]
  transfers between devices with their start and end apart: 2 -> 4, of which waited for: 2 -> 3; matrix products, arithmetic and copies ran while one was open for 9% -> 13% of each run, Pallas kernels for 0% -> 19%
where the time goes in v1:
time: 903 us; the launch traced here: 901 us
  waiting for transfers between devices  273 us (30%)
  Pallas kernels  254 us (28%)
  blocking collectives  208 us (23%)
  local copies, waits for them, and re-layouts  68.8 us (8%)
  other arithmetic  58.9 us (7%)
  starting transfers between devices  19.6 us (2%)
  between operations  18.5 us (2%)
    all_to_all x4, waiting for transfers between devices, exchange(): return lax.all_to_all(x, AXES, split_axis=0, concat_axis=0, tiled=True)  273 us
    all_to_all x3, blocking collectives, exchange(): return lax.all_to_all(x, AXES, split_axis=0, concat_axis=0, tiled=True)  208 us
    pallas_call x2, Pallas kernels, middle(): pl.pallas_call(functools.partial(middle_body, local), out_shape=[message]...  105 us
    pallas_call x2, Pallas kernels, last(): pl.pallas_call(functools.partial(last_body, local, count), out_shape=jax....  87.3 us
    pallas_call x2, Pallas kernels, pick(): pl.pallas_call(functools.partial(pick_body, chunk, local, parts), out_sha...  43.3 us
    another operation x2, other arithmetic, pair_kernel(): return jnp.stack([top, bottom], axis=0)  22.1 us
    all_to_all x4, starting transfers between devices, exchange(): return lax.all_to_all(x, AXES, split_axis=0, concat_axis=0, tiled=True)  19.6 us
    pallas_call x1, Pallas kernels, turn(): pl.pallas_call(turn_body, out_shape=jax.ShapeDtypeStruct((full * parts, L...  19.2 us
  transfers between devices with their start and end apart: 4, of which 3 were waited for; matrix products, arithmetic and copies ran while one was open for 13% of the time, Pallas kernels for 19%

profile of v1, /device:TPU:0, one launch (start us, length us, event | category | flops | bytes accessed | tf_op | source)
XLA Modules:
  0.0 901.5 jit_solution(854513996234486953)
XLA Ops:
  0.6 2.1 fusion.8
  2.7 1.6 fusion.9
  12.4 19.2 %turn.1.x_ref = f32[32768,128]{1,0:T(8,128)} custom-call(f32[512,8192]{1,0:T(8,128)} %bitcast.60), custom_call_target="tpu_custom_call" | custom-call | flops 100000000 | bytes 33554432 | tf_op jit(solution)/shard_map/turn/pallas_call | solution.py:206
  31.6 0.7 multiply_add_fusion.2.idx_ref
  32.3 21.6 %pick.2 = f32[32,512,128]{2,1,0:T(8,128)} custom-call(s32[8192]{0:T(1024)} %multiply_add_fusion.2.idx_ref, f32[32768,128]{1,0:T(8,128)} %turn.1.x_ref), custom_call_target="tpu_custom_call" | custom-call | flops 100000000 | bytes 50331648 | tf_op jit(solution)/shard_map/pick/pallas_call | solution.py:225
  53.9 7.5 all-to-all-start
  61.4 21.6 %pick.3 = f32[32,512,128]{2,1,0:T(8,128)} custom-call(s32[8192]{0:T(1024)} %multiply_add_fusion.2.idx_ref, f32[32768,128]{1,0:T(8,128)} %turn.1.x_ref), custom_call_target="tpu_custom_call" | custom-call | flops 100000000 | bytes 50331648 | tf_op jit(solution)/shard_map/pick/pallas_call | solution.py:225
  83.0 0.0 copy-start
  83.0 164.4 %all-to-all-done.r_ref = f32[32,512,128]{2,1,0:T(8,128)} async-done(((f32[32,512,128]{2,1,0:T(8,128)}), f32[32,512,128]{2,1,0:T(8,128)}, u32[]{:S(2)}, u32[]{:S(2)}) %all-to-all-start) | async-done | bytes 8388640 | tf_op jit(solution)/shard_map/all_to_all | solution.py:138
  247.5 4.4 all-to-all-start.1
  259.7 0.0 copy-done
  259.7 0.1 mul.416
  259.8 0.1 mul.420
  259.9 7.8 multiply_add_fusion
  267.7 7.8 add.151
  275.4 3.5 neg.21
  278.9 8.7 sub.36
  287.6 10.9 %maximum_bitcast_fusion.4 = (f32[1,16,16,2,16,16]{5,3,4,2,0,1:T(2,128)S(1)}, f32[1,16,16,2,16,16]{5,3,4,2,0,1:T(2,128)S(1)}) fusion(f32[16,16,1,16,16]{4,2,3,1,0:T(1,128)} %neg.21, f32[16,16,1,16,16]{4,2,3,1,0:T(1,128)} %sub.36, f32[16,16,1,16,16]{4,2,3,1,0:T(1,128)S(1)} %add.151), kind=kLoop, calls=%fused_computation.8 | loop fusion | flops 262144 | bytes 1835008 | tf_op jit(solution)/shard_map/stack | solution.py:134
  298.6 5.5 maximum_bitcast_fusion.1
  304.1 13.4 %reshape.363.w_ref = f32[512,512]{1,0:T(8,128)} reshape(f32[16,2,16,16,2,16]{5,4,3,2,1,0:T(2,128)} %maximum_bitcast_fusion.1) | data formatting | bytes 2097152 | tf_op jit(solution)/shard_map/reshape | solution.py:401
  317.4 0.7 fusion.2.next_ref
  318.2 52.3 %middle.2 = (f32[32,256,128]{2,1,0:T(8,128)}, f32[32,256,128]{2,1,0:T(8,128)}) custom-call(s32[8192]{0:T(1024)} %multiply_add_fusion.2.idx_ref, s32[8192]{0:T(1024)} %fusion.2.next_ref, f32[512,512]{1,0:T(8,128)} %reshape.363.w_ref, f32[32,512,128]{2,1,0:T(8,128)} %all-to-all-done.r_ref), custom_call_target="tpu_custom_call" | custom-call | flops 6442450944 | bytes 16777216 | tf_op jit(solution)/shard_map/middle/pallas_call | solution.py:303
  370.5 67.4 %all-to-all-done.1.r_ref = f32[32,512,128]{2,1,0:T(8,128)} async-done(((f32[32,512,128]{2,1,0:T(8,128)}), f32[32,512,128]{2,1,0:T(8,128)}, u32[]{:S(2)}, u32[]{:S(2)}) %all-to-all-start.1) | async-done | bytes 8388640 | tf_op jit(solution)/shard_map/all_to_all | solution.py:138
  437.9 98.0 %all_to_all.39.refs_0_ = f32[32,256,128]{2,1,0:T(8,128)} all-to-all(f32[32,256,128]{2,1,0:T(8,128)} %get-tuple-element.14), channel_id=1, replica_groups=mesh['hi'=16,'grp'=2] {'hi','grp'}, dimensions={0} | all-to-all | bytes 8388608 | tf_op jit(solution)/shard_map/all_to_all | solution.py:138
  535.9 3.8 all-to-all-start.3
  539.7 52.3 %middle.3 = (f32[32,256,128]{2,1,0:T(8,128)}, f32[32,256,128]{2,1,0:T(8,128)}) custom-call(s32[8192]{0:T(1024)} %multiply_add_fusion.2.idx_ref, s32[8192]{0:T(1024)} %fusion.2.next_ref, f32[512,512]{1,0:T(8,128)} %reshape.363.w_ref, f32[32,512,128]{2,1,0:T(8,128)} %all-to-all-done.1.r_ref), custom_call_target="tpu_custom_call" | custom-call | flops 6442450944 | bytes 16777216 | tf_op jit(solution)/shard_map/middle/pallas_call | solution.py:303
  592.0 41.6 %all-to-all-done.3.refs_0_ = f32[32,256,128]{2,1,0:T(8,128)} async-done(((f32[32,256,128]{2,1,0:T(8,128)}), f32[32,256,128]{2,1,0:T(8,128)}, u32[]{:S(2)}, u32[]{:S(2)}) %all-to-all-start.3) | async-done | bytes 4194336 | tf_op jit(solution)/shard_map/all_to_all | solution.py:138
  633.6 97.4 %all_to_all.40.refs_1_ = f32[32,256,128]{2,1,0:T(8,128)} all-to-all(f32[32,256,128]{2,1,0:T(8,128)} %get-tuple-element.18), channel_id=1, replica_groups=mesh['hi'=16,'grp'=2] {'hi','grp'}, dimensions={0} | all-to-all | bytes 8388608 | tf_op jit(solution)/shard_map/all_to_all | solution.py:138
  731.0 4.0 all-to-all-start.5
  735.0 0.1 mul.378
  735.0 0.2 copy.18
  735.3 0.1 mul.382
  735.3 0.2 copy.20
  735.5 7.8 multiply_add_fusion.1
  743.4 7.8 add.135
  751.1 3.5 neg.20
  754.6 8.7 sub.33
  763.3 11.1 %maximum_bitcast_fusion.2 = (f32[1,16,16,2,16,16]{4,3,5,1,0,2:T(2,128)S(1)}, f32[1,16,16,2,16,16]{4,3,5,1,0,2:T(2,128)S(1)}) fusion(f32[16,16,1,16,16]{3,2,4,0,1:T(1,128)} %neg.20, f32[16,16,1,16,16]{3,2,4,0,1:T(1,128)} %sub.33, f32[16,16,1,16,16]{3,2,4,0,1:T(1,128)S(1)} %add.135), kind=kLoop, calls=%fused_computation.6 | loop fusion | flops 262144 | bytes 1835008 | tf_op jit(solution)/shard_map/stack | solution.py:134
  774.5 5.5 maximum_bitcast_fusion
  780.0 13.3 %reshape.362.w_ref = f32[512,512]{1,0:T(8,128)} reshape(f32[16,2,16,16,2,16]{5,4,3,2,1,0:T(2,128)} %maximum_bitcast_fusion) | data formatting | bytes 2097152 | tf_op jit(solution)/shard_map/reshape | solution.py:402
  793.3 0.7 multiply_add_fusion.3.idx_ref
  794.0 43.6 %last.2.refs_2_ = f32[2,256,8192]{2,1,0:T(8,128)} custom-call(s32[8192]{0:T(1024)} %multiply_add_fusion.3.idx_ref, f32[512,512]{1,0:T(8,128)} %reshape.362.w_ref, f32[32,256,128]{2,1,0:T(8,128)} %all_to_all.39.refs_0_, f32[32,256,128]{2,1,0:T(8,128)} %all_to_all.40.refs_1_), custom_call_target="tpu_custom_call" | custom-call | flops 6442450944 | bytes 33554432 | tf_op jit(solution)/shard_map/last/pallas_call | solution.py:364
  837.6 0.0 all-to-all-done.5.refs_1_
  837.6 43.7 %last.3 = f32[2,256,8192]{2,1,0:T(8,128)} custom-call(s32[8192]{0:T(1024)} %multiply_add_fusion.3.idx_ref, f32[512,512]{1,0:T(8,128)} %reshape.362.w_ref, f32[32,256,128]{2,1,0:T(8,128)} %all-to-all-done.3.refs_0_, f32[32,256,128]{2,1,0:T(8,128)} %all-to-all-done.5.refs_1_, f32[2,256,8192]{2,1,0:T(8,128)} %last.2.refs_2_), custom_call_target="tpu_custom_call", output_to_operand_aliasing={{}: (4, {})} | custom-call | flops 6442450944 | bytes 33554432 | tf_op jit(solution)/shard_map/last/pallas_call | solution.py:364
  881.3 3.9 slice.192
  885.2 0.6 fusion
  885.9 0.7 broadcast_in_dim.8
  886.5 12.6 %all_to_all.41 = f32[32,1,128]{2,1,0:T(1,128)S(1)} all-to-all(f32[32,1,128]{2,1,0:T(1,128)S(1)} %broadcast_in_dim.8), channel_id=1, replica_groups=mesh['hi'=16,'grp'=2] {'hi','grp'}, dimensions={0} | all-to-all | bytes 32768 | tf_op jit(solution)/shard_map/all_to_all | solution.py:138
  899.1 0.6 slice_reduce_fusion
  (1 shorter events, 0.0 us)
Async XLA Ops:
  53.9 193.5 %all-to-all-start = ((f32[32,512,128]{2,1,0:T(8,128)}), f32[32,512,128]{2,1,0:T(8,128)}, u32[]{:S(2)}, u32[]{:S(2)}) async-start(f32[32,512,128]{2,1,0:T(8,128)} %pick.2), calls=%async_computation | async-start | bytes 16777216 | tf_op jit(solution)/shard_map/all_to_all | solution.py:138
  83.0 176.7 %copy-start = (f32[2,2,16,16]{3,2,1,0:T(8,128)S(1)}, f32[2,2,16,16]{3,2,1,0:T(8,128)}, u32[]{:S(2)}) copy-start(f32[2,2,16,16]{3,2,1,0:T(8,128)} %param.5) | copy-start | bytes 12292
  247.5 190.5 %all-to-all-start.1 = ((f32[32,512,128]{2,1,0:T(8,128)}), f32[32,512,128]{2,1,0:T(8,128)}, u32[]{:S(2)}, u32[]{:S(2)}) async-start(f32[32,512,128]{2,1,0:T(8,128)} %pick.3), calls=%async_computation.1 | async-start | bytes 16777216 | tf_op jit(solution)/shard_map/all_to_all | solution.py:138
  535.9 97.6 %all-to-all-start.3 = ((f32[32,256,128]{2,1,0:T(8,128)}), f32[32,256,128]{2,1,0:T(8,128)}, u32[]{:S(2)}, u32[]{:S(2)}) async-start(f32[32,256,128]{2,1,0:T(8,128)} %get-tuple-element.15), calls=%async_computation.3 | async-start | bytes 8388608 | tf_op jit(solution)/shard_map/all_to_all | solution.py:138
  731.0 106.7 %all-to-all-start.5 = ((f32[32,256,128]{2,1,0:T(8,128)}), f32[32,256,128]{2,1,0:T(8,128)}, u32[]{:S(2)}, u32[]{:S(2)}) async-start(f32[32,256,128]{2,1,0:T(8,128)} %get-tuple-element.19), calls=%async_computation.5 | async-start | bytes 8388608 | tf_op jit(solution)/shard_map/all_to_all | solution.py:138
